TPU v7x, 256 devices: a whole 4x4x8 slice. The times are simulated.
256 devices in a mesh: gz: 8 (over z_hi, y), xy: 32 (over z_lo, x, core).
Axes of the slice: x: 4, y: 4, z: 8 (z_hi: 2, z_lo: 4; z = z_hi * 4 + z_lo), core: 2. Of those that a mesh axis runs over, the one named last changes fastest.
Arguments:
- stack: bfloat16 [128, 512, 2048], P('gz', 'xy'), may hold values from -8 to 8
Outputs:
- joined: float32 [512, 2048], P('xy', 'gz')
- pooled: float32 [256, 1024], P('xy', 'gz')
All inputs are finite; a program needn't handle non-finite values.
Results may differ from a plain program's by a relative error of at most 0.0003.
Values may be sent and summed in bfloat16 or wider, within the bound.
No kernel may reach another device: no remote copies, remote signals or barrier semaphores. Data moves between devices by JAX's collectives and lax.ppermute only.
A program may use at most 128 MiB of HBM per device.

v0:
```python
import jax
import jax.numpy as jnp
from jax import lax
from jax.sharding import PartitionSpec as P

sharpness = 0.016
laplace_taps = (
    (0, 0, 16.0),
    (1, 0, -2.0),
    (-1, 0, -2.0),
    (0, 1, -2.0),
    (0, -1, -2.0),
    (1, 1, -1.0),
    (1, -1, -1.0),
    (-1, 1, -1.0),
    (-1, -1, -1.0),
    (2, 0, -1.0),
    (-2, 0, -1.0),
    (0, 2, -1.0),
    (0, -2, -1.0),
)


def with_halo(cells, sides, width):
    for axis, dim in sides:
        count = lax.axis_size(axis)
        ends = count - 1
        head = lax.slice_in_dim(cells, 0, width, axis=dim)
        tail = lax.slice_in_dim(cells, cells.shape[dim] - width, cells.shape[dim], axis=dim)
        cells = jnp.concatenate(
            [
                lax.ppermute(tail, axis, [(i, (i + 1) % count) for i in range(ends)]),
                cells,
                lax.ppermute(head, axis, [((i + 1) % count, i) for i in range(ends)]),
            ],
            axis=dim,
        )
    return cells


def in_one_piece(arrays, axis, split_dim, concat_dim, along):
    widths = [a.shape[along] for a in arrays]
    both = jnp.concatenate(arrays, axis=along)
    out = lax.all_to_all(both, axis, split_axis=split_dim, concat_axis=concat_dim, tiled=True)
    return tuple(jnp.split(out, [sum(widths[:k]) for k in range(1, len(widths))], axis=along))


def column_shift(values, col_step):
    if col_step == 0:
        return values
    breadth = values.shape[-1]
    if col_step > 0:
        return jnp.pad(values[..., col_step:], ((0, 0), (0, 0), (0, col_step)))
    return jnp.pad(values[..., : breadth + col_step], ((0, 0), (0, 0), (-col_step, 0)))


def laplace_rows(padded, out_rows):
    total = None
    for row_step, col_step, weight in laplace_taps:
        rows_view = padded[:, 2 + row_step : 2 + row_step + out_rows, :].astype(jnp.float32)
        term = weight * column_shift(rows_view, col_step)
        total = term if total is None else total + term
    return total


def box_rows(padded, out_rows):
    row_total = padded[:, 0:out_rows, :]
    for shift_amount in range(-1, 3):
        row_total = row_total + padded[:, 2 + shift_amount : 2 + shift_amount + out_rows, :]
    box_total = column_shift(row_total, -2)
    for shift_amount in range(-1, 3):
        box_total = box_total + column_shift(row_total, shift_amount)
    return box_total


def shards(stack):
    row_count = stack.shape[1]
    col_count = stack.shape[2]
    rimmed = with_halo(stack, (("xy", 1),), 2)
    laplace_out = laplace_rows(rimmed, row_count)
    energy = laplace_out * laplace_out
    energy_wide = with_halo(energy, (("xy", 1),), 2)
    score = box_rows(energy_wide, row_count) * sharpness
    local_max = jnp.max(score, axis=0)
    weights = jnp.exp(score - local_max[None, :, :])
    weighted_sum = jnp.sum(weights * stack.astype(jnp.float32), axis=0)
    weight_sum = jnp.sum(weights, axis=0)
    own_cols = col_count // lax.axis_size("gz")
    group_max, group_weighted, group_weights = in_one_piece(
        (local_max[None], weighted_sum[None], weight_sum[None]), "gz", 2, 0, 1
    )
    joint_max = jnp.max(group_max, axis=0)
    rescale = jnp.exp(group_max - joint_max[None])
    own_weighted = jnp.sum(group_weighted * rescale, axis=0)
    own_weights = jnp.sum(group_weights * rescale, axis=0)
    joined = own_weighted / own_weights
    pooled = joined.reshape(row_count // 2, 2, own_cols // 2, 2).mean(axis=(1, 3))
    return (joined, pooled)


def solution(mesh):
    in_specs = (P("gz", "xy", None),)
    out_specs = (P("xy", "gz"), P("xy", "gz"))
    return jax.shard_map(shards, mesh=mesh, in_specs=in_specs, out_specs=out_specs, check_vma=False)
```

profile of v0, /device:TPU:32, one launch (start us, length us, event | category | flops | bytes accessed | tf_op | source)
XLA Modules:
  0.0 81.8 jit_solution(6715013422025656606)
XLA Ops:
  0.6 1.4 %fusion.17 = (bf16[16,2,2048]{2,1,0:T(2,128)(2,1)S(1)}, bf16[16,2,2048]{2,1,0:T(2,128)(2,1)S(1)}) fusion(bf16[16,16,2048]{2,1,0:T(8,128)(2,1)} %param.1), kind=kLoop, calls=%fused_computation.40 | loop fusion | bytes 524288 | tf_op jit(solution)/shard_map/slice | solution.py:28
  2.1 1.9 %collective-permute-start.1 = (bf16[16,2,2048]{2,0,1:T(8,128)(2,1)S(1)}, bf16[16,2,2048]{2,0,1:T(8,128)(2,1)S(1)}, u32[]{:S(2)}, u32[]{:S(2)}) collective-permute-start(bf16[16,2,2048]{2,0,1:T(8,128)(2,1)S(1)} %copy.22), channel_id=1, source_target_pairs={{0,1},{1,2},{2,3},{3,4},{4,5},{5,6},{6,7},{7,8},{8,9},{9,10},{10,1... | collective-permute-start | bytes 393224 | tf_op jit(solution)/shard_map/ppermute | solution.py:32
  4.1 5.8 %collective-permute-start = (bf16[16,2,2048]{2,0,1:T(8,128)(2,1)S(1)}, bf16[16,2,2048]{2,0,1:T(8,128)(2,1)S(1)}, u32[]{:S(2)}, u32[]{:S(2)}) collective-permute-start(bf16[16,2,2048]{2,0,1:T(8,128)(2,1)S(1)} %copy.23), channel_id=1, source_target_pairs={{1,0},{2,1},{3,2},{4,3},{5,4},{6,5},{7,6},{8,7},{9,8},{10,9},{11,1... | collective-permute-start | bytes 393224 | tf_op jit(solution)/shard_map/ppermute | solution.py:34
  9.8 0.7 collective-permute-done.1
  10.5 1.9 %constant_dynamic-update-slice_fusion.1 = (bf16[16,18,2048]{2,0,1:T(8,128)(2,1)S(1)}, f32[16,16,2048]{2,0,1:T(8,128)S(1)}, bf16[16,18,2048]{2,0,1:T(8,128)(2,1)S(1)}) fusion(bf16[16,16,2048]{2,1,0:T(8,128)(2,1)} %param.1, bf16[16,18,2048]{2,0,1:T(8,128)(2,1)S(1)} %constant_dynamic-update-slice_fusion.3), kind=kLoop, calls=%fused_computation.27 | loop fusion | flops 524287 | bytes 5242880
  12.4 0.2 slice_convert_fusion
  12.7 1.7 %fusion.13 = (f32[16,16,2047]{2,0,1:T(8,128)S(1)}, f32[16,16,2047]{2,0,1:T(8,128)S(1)}, f32[16,16,2047]{2,0,1:T(8,128)S(1)}, f32[16,16,2047]{2,0,1:T(8,128)S(1)}) fusion(f32[16,16,2048]{2,0,1:T(8,128)S(1)} %get-tuple-element.27, f32[16,16,2048]{2,0,1:T(8,128)S(1)} %slice_convert_fusion), kind=kLoop, calls=%fused_computation.36 | loop fusion | bytes 16769024 | tf_op jit(solution)/shard_map/slice | solution.py:53
  14.4 0.8 fusion.16
  15.2 0.2 slice_convert_fusion.1
  15.5 0.8 fusion.14
  16.3 0.4 copy-done
  16.7 5.5 %add_multiply_fusion.1 = f32[16,16,2048]{2,0,1:T(8,128)S(1)} fusion(f32[16,16,2046]{2,0,1:T(8,128)S(1)} %get-tuple-element.23, f32[16,16,2046]{2,0,1:T(8,128)S(1)} %get-tuple-element.22, f32[16,16,2047]{2,0,1:T(8,128)S(1)} %get-tuple-element.29, f32[16,16,2047]{2,0,1:T(8,128)S(1)} %get-tuple-element.30, f32[16,16,2047]{2,0,1:T(8,128)S(1)} %get-tuple-element.19, ...), kind=kLoop, calls=%fused_computation.15 | loop fusion | flops 16252928 | bytes 24107008 | tf_op jit(solution)/shard_map/mul | solution.py:81
  22.2 1.9 %collective-permute-start.2 = (f32[16,2,2048]{2,0,1:T(8,128)S(1)}, f32[16,2,2048]{2,0,1:T(8,128)S(1)}, u32[]{:S(2)}, u32[]{:S(2)}) collective-permute-start(f32[16,2,2048]{2,0,1:T(8,128)S(1)} %get-tuple-element.14), channel_id=1, source_target_pairs={{0,1},{1,2},{2,3},{3,4},{4,5},{5,6},{6,7},{7,8},{8,9},{9,10},{10,1... | collective-permute-start | bytes 786440 | tf_op jit(solution)/shard_map/ppermute | solution.py:32
  24.1 5.9 %collective-permute-start.3 = (f32[16,2,2048]{2,0,1:T(8,128)S(1)}, f32[16,2,2048]{2,0,1:T(8,128)S(1)}, u32[]{:S(2)}, u32[]{:S(2)}) collective-permute-start(f32[16,2,2048]{2,0,1:T(8,128)S(1)} %get-tuple-element.15), channel_id=1, source_target_pairs={{1,0},{2,1},{3,2},{4,3},{5,4},{6,5},{7,6},{8,7},{9,8},{10,9},{11,1... | collective-permute-start | bytes 786440 | tf_op jit(solution)/shard_map/ppermute | solution.py:34
  30.1 1.9 %collective-permute-done.2 = f32[16,2,2048]{2,0,1:T(8,128)S(1)} collective-permute-done((f32[16,2,2048]{2,0,1:T(8,128)S(1)}, f32[16,2,2048]{2,0,1:T(8,128)S(1)}, u32[]{:S(2)}, u32[]{:S(2)}) %collective-permute-start.2) | collective-permute-done | bytes 262176 | tf_op jit(solution)/shard_map/ppermute | solution.py:32
  32.0 1.8 %collective-permute-done.3 = f32[16,2,2048]{2,0,1:T(8,128)S(1)} collective-permute-done((f32[16,2,2048]{2,0,1:T(8,128)S(1)}, f32[16,2,2048]{2,0,1:T(8,128)S(1)}, u32[]{:S(2)}, u32[]{:S(2)}) %collective-permute-start.3) | collective-permute-done | bytes 262176 | tf_op jit(solution)/shard_map/ppermute | solution.py:34
  33.7 0.9 %fusion.2 = f32[16,16,2048]{2,0,1:T(8,128)S(1)} fusion(f32[16,16,2048]{2,0,1:T(8,128)S(1)} %add_multiply_fusion.1, f32[16,2,2048]{2,0,1:T(8,128)S(1)} %collective-permute-done.3, f32[16,2,2048]{2,0,1:T(8,128)S(1)} %collective-permute-done.2), kind=kLoop, calls=%fused_computation.6 | loop fusion | flops 4194304 | bytes 4718592 | tf_op jit(solution)/shard_map/add | solution.py:69
  34.6 0.8 fusion.10
  35.4 0.8 fusion.11
  36.2 1.5 %fusion.9 = (f32[16,2048]{1,0:T(8,128)S(1)}, f32[16,16,2048]{2,0,1:T(8,128)S(1)}) fusion(f32[16,16,2046]{2,0,1:T(8,128)S(1)} %get-tuple-element.11, f32[16,16,2047]{2,0,1:T(8,128)S(1)} %get-tuple-element.13, f32[16,16,2048]{2,0,1:T(8,128)S(1)} %fusion.2, f32[16,16,2047]{2,0,1:T(8,128)S(1)} %get-tuple-element.12, f32[16,16,2046]{2,0,1:T(8,128)S(1)} %get-tuple-element.10), kind=kLoop, calls=%fused_computation.32 | loop fusion | flops 3112960 | bytes 12707840 | tf_op jit(solution)/shard_map/reduce_max | solution.py:84
  37.7 1.3 %multiply_reduce_fusion = (f32[16,2048]{1,0:T(8,128)S(1)}, f32[16,2048]{1,0:T(8,128)S(1)}) fusion(f32[16,16,2048]{2,0,1:T(8,128)S(1)} %get-tuple-element.9, f32[16,2048]{1,0:T(8,128)S(1)} %get-tuple-element.8, bf16[16,16,2048]{2,1,0:T(8,128)(2,1)S(1)} %copy-done), kind=kLoop, calls=%fused_computation.12 | loop fusion | flops 2555904 | bytes 3538944 | tf_op jit(solution)/shard_map/reduce_sum | solution.py:86
  39.1 0.6 copy.14
  39.7 0.5 broadcast.37
  40.2 9.3 %reduce = f32[2048,48]{1,0:T(8,128)S(1)} reduce(f32[2048,1,48]{2,1,0:T(1,128)S(1)} %bitcast.12, f32[]{:T(128)} %broadcast.37), dimensions={1}, to_apply=%bitcast.8.reduce_sub_computation | reduce | bytes 786436
  49.5 1.0 %reshape.10 = f32[8,1,12288]{2,1,0:T(1,128)S(1)} reshape(f32[2048,48]{1,0:T(8,128)S(1)} %reduce) | data formatting | bytes 786432
  50.5 24.8 %all_to_all.18 = f32[8,1,12288]{2,1,0:T(1,128)S(1)} all-to-all(f32[8,1,12288]{2,1,0:T(1,128)S(1)} %reshape.10), channel_id=1, replica_groups=mesh['gz'=8,'xy'=32] {'gz'}, dimensions={0} | all-to-all | bytes 786432 | tf_op jit(solution)/shard_map/all_to_all | solution.py:44
  75.3 1.6 %reduce.1 = f32[8,12288]{1,0:T(8,128)S(1)} reduce(f32[8,1,12288]{2,1,0:T(1,128)S(1)} %all_to_all.18, f32[]{:T(128)} %broadcast.37), dimensions={1}, to_apply=%all_to_all.13.reduce_sub_computation | reduce | bytes 786436 | tf_op jit(solution)/shard_map/all_to_all | solution.py:44
  76.9 2.2 %reshape.11 = f32[2048,1,48]{2,1,0:T(1,128)S(1)} reshape(f32[8,12288]{1,0:T(8,128)S(1)} %reduce.1) | data formatting | bytes 786432
  79.2 0.6 fusion.7
  79.9 1.0 %div.14 = f32[8,2,128,2]{3,2,1,0:T(8,128)S(1)} reshape(f32[16,256]{1,0:T(8,128)S(1)} %copy.16) | data formatting | bytes 32768 | tf_op jit(solution)/shard_map/div | solution.py:96
  80.9 0.2 reduce_sum.49
  81.2 0.6 broadcast_multiply_fusion
  (13 shorter events, 0.3 us)
Async XLA Ops:
  2.1 8.4 %collective-permute-start.1 = (bf16[16,2,2048]{2,0,1:T(8,128)(2,1)S(1)}, bf16[16,2,2048]{2,0,1:T(8,128)(2,1)S(1)}, u32[]{:S(2)}, u32[]{:S(2)}) collective-permute-start(bf16[16,2,2048]{2,0,1:T(8,128)(2,1)S(1)} %copy.22), channel_id=1, source_target_pairs={{0,1},{1,2},{2,3},{3,4},{4,5},{5,6},{6,7},{7,8},{8,9},{9,10},{10,1... | collective-permute-start | bytes 393224 | tf_op jit(solution)/shard_map/ppermute | solution.py:32
  4.1 11.1 %collective-permute-start = (bf16[16,2,2048]{2,0,1:T(8,128)(2,1)S(1)}, bf16[16,2,2048]{2,0,1:T(8,128)(2,1)S(1)}, u32[]{:S(2)}, u32[]{:S(2)}) collective-permute-start(bf16[16,2,2048]{2,0,1:T(8,128)(2,1)S(1)} %copy.23), channel_id=1, source_target_pairs={{1,0},{2,1},{3,2},{4,3},{5,4},{6,5},{7,6},{8,7},{9,8},{10,9},{11,1... | collective-permute-start | bytes 393224 | tf_op jit(solution)/shard_map/ppermute | solution.py:34
  15.4 1.2 %copy-start = (bf16[16,16,2048]{2,1,0:T(8,128)(2,1)S(1)}, bf16[16,16,2048]{2,1,0:T(8,128)(2,1)}, u32[]{:S(2)}) copy-start(bf16[16,16,2048]{2,1,0:T(8,128)(2,1)} %param.1) | copy-start | bytes 3145732
  22.2 9.8 %collective-permute-start.2 = (f32[16,2,2048]{2,0,1:T(8,128)S(1)}, f32[16,2,2048]{2,0,1:T(8,128)S(1)}, u32[]{:S(2)}, u32[]{:S(2)}) collective-permute-start(f32[16,2,2048]{2,0,1:T(8,128)S(1)} %get-tuple-element.14), channel_id=1, source_target_pairs={{0,1},{1,2},{2,3},{3,4},{4,5},{5,6},{6,7},{7,8},{8,9},{9,10},{10,1... | collective-permute-start | bytes 786440 | tf_op jit(solution)/shard_map/ppermute | solution.py:32
  24.1 9.6 %collective-permute-start.3 = (f32[16,2,2048]{2,0,1:T(8,128)S(1)}, f32[16,2,2048]{2,0,1:T(8,128)S(1)}, u32[]{:S(2)}, u32[]{:S(2)}) collective-permute-start(f32[16,2,2048]{2,0,1:T(8,128)S(1)} %get-tuple-element.15), channel_id=1, source_target_pairs={{1,0},{2,1},{3,2},{4,3},{5,4},{6,5},{7,6},{8,7},{9,8},{10,9},{11,1... | collective-permute-start | bytes 786440 | tf_op jit(solution)/shard_map/ppermute | solution.py:34
  79.9 1.8 %copy-start.1 = (f32[16,256]{1,0:T(8,128)}, f32[16,256]{1,0:T(8,128)S(1)}, u32[]{:S(2)}) copy-start(f32[16,256]{1,0:T(8,128)S(1)} %copy.16) | copy-start | bytes 49156
where the time goes:
time: 82.1 us; the launch traced here: 81.8 us
  blocking collectives  24.8 us (30%)
  other arithmetic  24 us (29%)
  starting transfers between devices  15.5 us (19%)
  local copies, waits for them, and re-layouts  12.2 us (15%)
  waiting for transfers between devices  4.35 us (5%)
  between operations  0.88 us (1%)
    all_to_all x1, blocking collectives, in_one_piece(): lax.all_to_all(both, axis, split_axis=split_dim, concat_axis=concat_dim,...  24.8 us
    ppermute x2, starting transfers between devices, with_halo(): lax.ppermute(head, axis, [((i + 1) % count, i) for i in range(ends)])  11.7 us
    unnamed x2, other arithmetic  11.3 us
    mul x1, other arithmetic, shards(): energy = laplace_out * laplace_out  5.45 us
    unnamed x11, local copies, waits for them, and re-layouts  4.28 us
    ppermute x2, starting transfers between devices, with_halo(): lax.ppermute(tail, axis, [(i, (i + 1) % count) for i in range(ends)])  3.84 us
    slice x3, local copies, waits for them, and re-layouts, column_shift(): return jnp.pad(values[..., col_step:], ((0, 0), (0, 0), (0, col_step)))  3.29 us
    ppermute x2, waiting for transfers between devices, with_halo(): lax.ppermute(tail, axis, [(i, (i + 1) % count) for i in range(ends)])  2.59 us
  transfers between devices with their start and end apart: 4, of which 3 were waited for; matrix products, arithmetic and copies ran while one was open for 6% of the time, Pallas kernels for 0%

commit v1 on v0

v1 whole, which is shorter than its diff:
```python
import functools

import jax
import jax.numpy as jnp
from jax import lax
from jax.experimental import pallas as pl
from jax.experimental.pallas import tpu as pltpu
from jax.sharding import PartitionSpec as P

sharpness = 0.016
log2e = 1.4426950408889634
LANES = 128
HALO = 4


def shifted(tiles, step, lane, before=None):
    turned = [pltpu.roll(t, (-step) % LANES, axis=1) for t in tiles]
    blank = jnp.zeros_like(tiles[0])
    out = []
    for j in range(len(tiles)):
        if step > 0:
            other = turned[j + 1] if j + 1 < len(tiles) else blank
            out.append(jnp.where(lane < LANES - step, turned[j], other))
        else:
            other = turned[j - 1] if j > 0 else (blank if before is None else before)
            out.append(jnp.where(lane >= -step, turned[j], other))
    return out


def energy_row(load, count, lane):
    mids, cores, bases = [], [], []
    for j in range(count):
        core = load(2, j)
        near = load(1, j) + load(3, j)
        far = load(0, j) + load(4, j)
        mid = (core + core) + near
        mids.append(mid)
        cores.append(core)
        bases.append(20.0 * core - (mid + mid) - far)
    up1, down1 = shifted(mids, 1, lane), shifted(mids, -1, lane)
    up2, down2 = shifted(cores, 2, lane), shifted(cores, -2, lane)
    out = []
    for j in range(count):
        lap = bases[j] - (up1[j] + down1[j]) - (up2[j] + down2[j])
        out.append(lap * lap)
    return out


def partials_row(energy, cells, count, lane):
    cols = []
    for j in range(count):
        cols.append(((energy(0, j) + energy(1, j)) + (energy(3, j) + energy(4, j))) + energy(2, j))
    pairs = [a + b for a, b in zip(cols, shifted(cols, 1, lane))]
    before = jnp.where(lane == 1, pltpu.roll(cols[0], 1, axis=1), 0.0)
    fours = [a + b for a, b in zip(pairs, shifted(pairs, -2, lane, before))]
    fives = [a + b for a, b in zip(fours, shifted(cols, 2, lane))]
    out = []
    for j in range(count):
        score = fives[j] * (sharpness * log2e)
        top = jnp.max(score, axis=0, keepdims=True)
        weight = jnp.exp2(score - top)
        total = jnp.sum(weight, axis=0, keepdims=True)
        blend = jnp.sum(weight * cells(j), axis=0, keepdims=True)
        out.append((top, total, blend))
    return out


def tile(j):
    return pl.ds(j * LANES, LANES)


def turn_kernel(x_ref, xt_ref, a_ref, b_ref, swap, *, chunk):
    planes, rows, cols = x_ref.shape
    n = planes * rows
    o = lax.broadcasted_iota(jnp.int32, (n, n), 0)
    i = lax.broadcasted_iota(jnp.int32, (n, n), 1)
    hit = (o // planes == i % rows) & (o % planes == i // rows)
    swap[...] = jnp.where(hit, 1.0, 0.0).astype(jnp.bfloat16)
    odd = lax.rem(lax.axis_index("xy"), 2)
    last = rows - HALO
    for c in range(cols // chunk):
        ds = pl.ds(c * chunk, chunk)
        x = x_ref[:, :, ds].reshape(n, chunk)
        y = jnp.dot(swap[...], x, preferred_element_type=jnp.float32)
        xt_ref[:, :, ds] = y.reshape(rows, planes, chunk)
    a_ref[...] = xt_ref[pl.ds(last - odd * last, HALO)].astype(jnp.bfloat16)
    b_ref[...] = xt_ref[pl.ds(odd * last, HALO)].astype(jnp.bfloat16)


def inner_kernel(xt_ref, edge_ref, part_ref, energy):
    rows, planes, cols = xt_ref.shape
    count = cols // LANES
    lane = lax.broadcasted_iota(jnp.int32, (planes, LANES), 1)

    def first(r, carry):
        row = energy_row(lambda k, j: xt_ref[r + k, :, tile(j)], count, lane)
        for j in range(count):
            energy[r, :, tile(j)] = row[j]
        return carry

    lax.fori_loop(0, rows - 4, first, 0)
    edge_ref[0:4] = energy[0:4]
    edge_ref[4:8] = energy[rows - 8:rows - 4]

    for r in range(rows - 8):
        row = partials_row(
            lambda k, j: energy[r + k, :, tile(j)], lambda j: xt_ref[r + 4, :, tile(j)], count, lane
        )
        for j in range(count):
            for q in range(3):
                part_ref[q, pl.ds(r, 1), tile(j)] = row[j][q]


def outer_kernel(xt_ref, a_ref, b_ref, edge_ref, inner_ref, out_ref, cells, energy, part):
    rows, planes, cols = xt_ref.shape
    count = cols // LANES
    lane = lax.broadcasted_iota(jnp.int32, (planes, LANES), 1)
    me = lax.axis_index("xy")
    odd = lax.rem(me, 2)
    cells[pl.ds(12 - 12 * odd, 4)] = a_ref[...].astype(jnp.float32)
    cells[pl.ds(12 * odd, 4)] = b_ref[...].astype(jnp.float32)
    cells[4:8] = xt_ref[0:4]
    cells[8:12] = xt_ref[rows - 4:rows]
    energy[4:8] = edge_ref[0:4]
    energy[8:12] = edge_ref[4:8]
    above = jnp.where(me > 0, 1.0, 0.0)
    below = jnp.where(me < lax.axis_size("xy") - 1, 1.0, 0.0)

    def first(i, carry):
        side, k0 = i // 4, lax.rem(i, 4)
        row = energy_row(lambda k, j: cells[8 * side + k0 + k, :, tile(j)], count, lane)
        outside = jnp.where(side == 0, jnp.where(k0 < 2, 1 - above, 0.0), jnp.where(k0 >= 2, 1 - below, 0.0))
        keep = 1.0 - outside
        for j in range(count):
            energy[12 * side + k0, :, tile(j)] = row[j] * keep
        return carry

    lax.fori_loop(0, 8, first, 0)
    part[:, 4:rows - 4, :] = inner_ref[...]

    for i in range(8):
        side, k0 = i // 4, i % 4
        base = 8 * side + k0
        row = partials_row(
            lambda k, j: energy[base + k, :, tile(j)], lambda j: cells[4 + 4 * side + k0, :, tile(j)], count, lane
        )
        for j in range(count):
            for q in range(3):
                part[q, pl.ds((rows - 4) * side + k0, 1), tile(j)] = row[j][q]
    groups, _, own = out_ref.shape
    for g in range(groups):
        ds = pl.ds(g * own, own)
        total = part[1, :, ds]
        out_ref[g, 0:rows, :] = part[0, :, ds] + jnp.log2(total)
        out_ref[g, rows:2 * rows, :] = part[2, :, ds] / total


def join_kernel(in_ref, joined_ref, pooled_ref):
    groups, twice, own = in_ref.shape
    rows = twice // 2
    logs = [in_ref[g, 0:rows, :] for g in range(groups)]
    top = functools.reduce(jnp.maximum, logs)
    weights = [jnp.exp2(v - top) for v in logs]
    total = functools.reduce(jnp.add, weights)
    blend = functools.reduce(jnp.add, [w * in_ref[g, rows:twice, :] for g, w in enumerate(weights)])
    joined = blend / total
    joined_ref[...] = joined
    r = lax.broadcasted_iota(jnp.int32, (rows // 2, rows), 0)
    c = lax.broadcasted_iota(jnp.int32, (rows // 2, rows), 1)
    row_pairs = jnp.where(c // 2 == r, 0.25, 0.0)
    r = lax.broadcasted_iota(jnp.int32, (own, own // 2), 0)
    c = lax.broadcasted_iota(jnp.int32, (own, own // 2), 1)
    col_pairs = jnp.where(r // 2 == c, 1.0, 0.0)
    exact = lax.Precision.HIGHEST
    halves = jnp.dot(row_pairs, joined, preferred_element_type=jnp.float32, precision=exact)
    pooled_ref[...] = jnp.dot(halves, col_pairs, preferred_element_type=jnp.float32, precision=exact)


def vmem(count):
    return [pl.BlockSpec(memory_space=pltpu.VMEM)] * count


def params(mib):
    return pltpu.CompilerParams(vmem_limit_bytes=mib << 20)


def shards(stack):
    planes, rows, cols = stack.shape
    f32, bf16 = jnp.float32, jnp.bfloat16
    sds = jax.ShapeDtypeStruct
    strip = sds((HALO, planes, cols), bf16)
    xt, to_a, to_b = pl.pallas_call(
        functools.partial(turn_kernel, chunk=512),
        out_shape=(sds((rows, planes, cols), f32), strip, strip),
        in_specs=vmem(1),
        out_specs=tuple(vmem(3)),
        scratch_shapes=[pltpu.VMEM((planes * rows, planes * rows), bf16)],
        compiler_params=params(8),
        cost_estimate=pl.CostEstimate(flops=10**7, bytes_accessed=4 << 20, transcendentals=0),
        name="turn",
    )(stack)
    count = lax.axis_size("xy")
    ends = [(i, i + 1) for i in range(1, count - 1, 2)]
    from_b = lax.ppermute(to_b, "xy", ends + [(j, i) for i, j in ends])
    from_a = lax.ppermute(to_a, "xy", [(i, i ^ 1) for i in range(count)])
    edge, inner = pl.pallas_call(
        inner_kernel,
        out_shape=(sds((8, planes, cols), f32), sds((3, rows - 8, cols), f32)),
        in_specs=vmem(1),
        out_specs=tuple(vmem(2)),
        scratch_shapes=[pltpu.VMEM((rows - 4, planes, cols), f32)],
        compiler_params=params(16),
        cost_estimate=pl.CostEstimate(flops=10**8, bytes_accessed=4 << 20, transcendentals=10**6),
        name="inner",
    )(xt)
    groups = lax.axis_size("gz")
    own = cols // groups
    ready = pl.pallas_call(
        outer_kernel,
        out_shape=sds((groups, 2 * rows, own), f32),
        in_specs=vmem(5),
        out_specs=vmem(1)[0],
        scratch_shapes=[
            pltpu.VMEM((16, planes, cols), f32),
            pltpu.VMEM((16, planes, cols), f32),
            pltpu.VMEM((3, rows, cols), f32),
        ],
        compiler_params=params(16),
        cost_estimate=pl.CostEstimate(flops=10**8, bytes_accessed=4 << 20, transcendentals=10**6),
        name="outer",
    )(xt, from_a, from_b, edge, inner)
    parts = lax.all_to_all(ready, "gz", split_axis=0, concat_axis=0, tiled=True)
    return pl.pallas_call(
        join_kernel,
        out_shape=(sds((rows, own), f32), sds((rows // 2, own // 2), f32)),
        in_specs=vmem(1),
        out_specs=tuple(vmem(2)),
        compiler_params=params(4),
        name="join",
    )(parts)


def solution(mesh):
    in_specs = (P("gz", "xy", None),)
    out_specs = (P("xy", "gz"), P("xy", "gz"))
    return jax.shard_map(shards, mesh=mesh, in_specs=in_specs, out_specs=out_specs, check_vma=False)
```

time: 82.1 us -> 39.4 us (0.48)
  other arithmetic: 24 us -> 0 us
  starting transfers between devices: 15.5 us -> 4.41 us
  local copies, waits for them, and re-layouts: 12.2 us -> 1.22 us
  Pallas kernels: 0 us -> 8.96 us
  waiting for transfers between devices: 4.35 us -> 1.46 us
  blocking collectives: 24.8 us -> 22.5 us
    unnamed x2 -> x0, other arithmetic: 11.3 us -> none
    ppermute x4 -> x2, starting transfers between devices: 15.5 us -> 4.41 us  [the longest x1 4.31 us: shards(): from_b = lax.ppermute(to_b, 'xy', ends + [(j, i) for i, j in ends])]
    pallas_call x0 -> x4, Pallas kernels: none -> 8.96 us  [the longest x1 4 us: shards(): pl.pallas_call(inner_kernel, out_shape=(sds((8, planes, cols), f32), sds(...]
    slice x7 -> x0, local copies, waits for them, and re-layouts: 6.26 us -> none  [the longest x3 3.29 us: column_shift(): return jnp.pad(values[..., col_step:], ((0, 0), (0, 0), (0, col_step)))]
    mul x1 -> x0, other arithmetic: 5.45 us -> none  [shards(): energy = laplace_out * laplace_out]
    unnamed x11 -> x2, local copies, waits for them, and re-layouts: 4.28 us -> 1.22 us
    ppermute x4 -> x2, waiting for transfers between devices: 4.35 us -> 1.46 us  [the longest x1 1.46 us: shards(): from_b = lax.ppermute(to_b, 'xy', ends + [(j, i) for i, j in ends])]
    all_to_all x1, blocking collectives: 24.8 us -> 22.5 us  [shards(): parts = lax.all_to_all(ready, 'gz', split_axis=0, concat_axis=0, tiled=True)]
  transfers between devices with their start and end apart: 4 -> 2, of which waited for: 3 -> 1; matrix products, arithmetic and copies ran while one was open for 6% -> 0% of each run, Pallas kernels for 0% -> 10%
where the time goes in v1:
time: 39.4 us; the launch traced here: 39.2 us
  blocking collectives  22.5 us (57%)
  Pallas kernels  8.96 us (23%)
  starting transfers between devices  4.41 us (11%)
  waiting for transfers between devices  1.46 us (4%)
  local copies, waits for them, and re-layouts  1.22 us (3%)
  between operations  0.68 us (2%)
    all_to_all x1, blocking collectives, shards(): parts = lax.all_to_all(ready, 'gz', split_axis=0, concat_axis=0, tiled=True)  22.5 us
    ppermute x1, starting transfers between devices, shards(): from_b = lax.ppermute(to_b, 'xy', ends + [(j, i) for i, j in ends])  4.31 us
    pallas_call x1, Pallas kernels, shards(): pl.pallas_call(inner_kernel, out_shape=(sds((8, planes, cols), f32), sds(...  4 us
    pallas_call x1, Pallas kernels, shards(): pl.pallas_call(outer_kernel, out_shape=sds((groups, 2 * rows, own), f32),...  3.47 us
    ppermute x1, waiting for transfers between devices, shards(): from_b = lax.ppermute(to_b, 'xy', ends + [(j, i) for i, j in ends])  1.46 us
    unnamed x2, local copies, waits for them, and re-layouts  1.22 us
    pallas_call x1, Pallas kernels, shards(): pl.pallas_call(join_kernel, out_shape=(sds((rows, own), f32), sds((rows /...  0.92 us
  transfers between devices with their start and end apart: 2, of which 1 were waited for; matrix products, arithmetic and copies ran while one was open for 0% of the time, Pallas kernels for 10%

profile of v1, /device:TPU:32, one launch (start us, length us, event | category | flops | bytes accessed | tf_op | source)
XLA Modules:
  0.0 39.2 jit_solution(8304386756868204897)
XLA Ops:
  0.6 0.0 copy-start
  0.6 1.2 %copy-done = bf16[16,16,2048]{2,1,0:T(8,128)(2,1)S(1)} copy-done((bf16[16,16,2048]{2,1,0:T(8,128)(2,1)S(1)}, bf16[16,16,2048]{2,1,0:T(8,128)(2,1)}, u32[]{:S(2)}) %copy-start) | copy-done | bytes 1048600
  1.9 0.6 %turn.1 = (f32[16,16,2048]{2,1,0:T(8,128)S(1)}, bf16[4,16,2048]{2,1,0:T(8,128)(2,1)S(1)}, bf16[4,16,2048]{2,1,0:T(8,128)(2,1)S(1)}) custom-call(bf16[16,16,2048]{2,1,0:T(8,128)(2,1)S(1)} %copy-done), custom_call_target="tpu_custom_call" | custom-call | flops 10000000 | bytes 4194304 | tf_op jit(solution)/shard_map/turn/pallas_call | solution.py:192
  2.4 0.1 collective-permute-start
  2.5 4.3 %collective-permute-start.1 = (bf16[4,16,2048]{2,1,0:T(8,128)(2,1)S(1)}, bf16[4,16,2048]{2,1,0:T(8,128)(2,1)S(1)}, u32[]{:S(2)}, u32[]{:S(2)}) collective-permute-start(bf16[4,16,2048]{2,1,0:T(8,128)(2,1)S(1)} %get-tuple-element.9), channel_id=1, source_target_pairs={{1,2},{3,4},{5,6},{7,8},{9,10},{11,12},{13,14},{15,16},{17,18},{19... | collective-permute-start | bytes 786440 | tf_op jit(solution)/shard_map/ppermute | solution.py:204
  6.8 4.0 %inner.1 = (f32[8,16,2048]{2,1,0:T(8,128)S(1)}, f32[3,8,2048]{2,1,0:T(8,128)S(1)}) custom-call(f32[16,16,2048]{2,1,0:T(8,128)S(1)} %get-tuple-element.7.xt_ref), custom_call_target="tpu_custom_call" | custom-call | flops 100000000 | bytes 4194304 | tf_op jit(solution)/shard_map/inner/pallas_call | solution.py:206
  10.9 0.0 collective-permute-done.a_ref
  10.9 1.5 %collective-permute-done.1.b_ref = bf16[4,16,2048]{2,1,0:T(8,128)(2,1)S(1)} collective-permute-done((bf16[4,16,2048]{2,1,0:T(8,128)(2,1)S(1)}, bf16[4,16,2048]{2,1,0:T(8,128)(2,1)S(1)}, u32[]{:S(2)}, u32[]{:S(2)}) %collective-permute-start.1) | collective-permute-done | bytes 262176 | tf_op jit(solution)/shard_map/ppermute | solution.py:204
  12.3 3.5 %outer.1 = f32[8,32,256]{2,1,0:T(8,128)S(1)} custom-call(f32[16,16,2048]{2,1,0:T(8,128)S(1)} %get-tuple-element.7.xt_ref, bf16[4,16,2048]{2,1,0:T(8,128)(2,1)S(1)} %collective-permute-done.a_ref, bf16[4,16,2048]{2,1,0:T(8,128)(2,1)S(1)} %collective-permute-done.1.b_ref, f32[8,16,2048]{2,1,0:T(8,128)S(1)} %get-tuple-element.10.edge_ref, ...), custom_call_target="tpu_custom_call" | custom-call | flops 100000000 | bytes 4194304 | tf_op jit(solution)/shard_map/outer/pallas_call | solution.py:218
  15.8 22.5 %all_to_all.5.in_ref = f32[8,32,256]{2,1,0:T(8,128)S(1)} all-to-all(f32[8,32,256]{2,1,0:T(8,128)S(1)} %outer.1), channel_id=1, replica_groups=mesh['gz'=8,'xy'=32] {'gz'}, dimensions={0} | all-to-all | bytes 524288 | tf_op jit(solution)/shard_map/all_to_all | solution.py:232
  38.3 0.9 %join.1 = (f32[16,256]{1,0:T(8,128)}, f32[8,128]{1,0:T(8,128)}) custom-call(f32[8,32,256]{2,1,0:T(8,128)S(1)} %all_to_all.5.in_ref), custom_call_target="tpu_custom_call" | custom-call | tf_op jit(solution)/shard_map/join/pallas_call | solution.py:233
Async XLA Ops:
  0.6 1.2 %copy-start = (bf16[16,16,2048]{2,1,0:T(8,128)(2,1)S(1)}, bf16[16,16,2048]{2,1,0:T(8,128)(2,1)}, u32[]{:S(2)}) copy-start(bf16[16,16,2048]{2,1,0:T(8,128)(2,1)} %x_ref.1) | copy-start | bytes 3145732
  2.4 8.4 %collective-permute-start = (bf16[4,16,2048]{2,1,0:T(8,128)(2,1)S(1)}, bf16[4,16,2048]{2,1,0:T(8,128)(2,1)S(1)}, u32[]{:S(2)}, u32[]{:S(2)}) collective-permute-start(bf16[4,16,2048]{2,1,0:T(8,128)(2,1)S(1)} %get-tuple-element.8), channel_id=1, source_target_pairs={{0,1},{1,0},{2,3},{3,2},{4,5},{5,4},{6,7},{7,6},{8,9},{9,8},{10,11... | collective-permute-start | bytes 786440 | tf_op jit(solution)/shard_map/ppermute | solution.py:205
  2.5 9.8 %collective-permute-start.1 = (bf16[4,16,2048]{2,1,0:T(8,128)(2,1)S(1)}, bf16[4,16,2048]{2,1,0:T(8,128)(2,1)S(1)}, u32[]{:S(2)}, u32[]{:S(2)}) collective-permute-start(bf16[4,16,2048]{2,1,0:T(8,128)(2,1)S(1)} %get-tuple-element.9), channel_id=1, source_target_pairs={{1,2},{3,4},{5,6},{7,8},{9,10},{11,12},{13,14},{15,16},{17,18},{19... | collective-permute-start | bytes 786440 | tf_op jit(solution)/shard_map/ppermute | solution.py:204

commit v2 on v1

v2 whole, which is shorter than its diff:
```python
import functools

import jax
import jax.numpy as jnp
from jax import lax
from jax.experimental import pallas as pl
from jax.experimental.pallas import tpu as pltpu
from jax.sharding import PartitionSpec as P


sharpness = 0.016
log2e = 1.4426950408889634
LANES = 128
HALO = 4
UNROLL = 2


def tile(j):
    return pl.ds(j * LANES, LANES)


def moved(turned, j, step, lane):
    if step > 0:
        other = turned[j + 1] if j + 1 < len(turned) else jnp.zeros_like(turned[j])
        return jnp.where(lane < LANES - step, turned[j], other)
    other = turned[j - 1] if j > 0 else jnp.zeros_like(turned[j])
    return jnp.where(lane >= -step, turned[j], other)


def rotated(tiles, step):
    return [pltpu.roll(t, (-step) % LANES, axis=1) for t in tiles]


def energy_row(load, count, lane):
    cells = [load(2, j) for j in range(count)]
    besides = [(c + c) + (load(1, j) + load(3, j)) for j, c in enumerate(cells)]
    up1, down1 = rotated(besides, 1), rotated(besides, -1)
    up2, down2 = rotated(cells, 2), rotated(cells, -2)
    for j in range(count):
        middle = (20.0 * cells[j] - (besides[j] + besides[j])) - (load(0, j) + load(4, j))
        lap = (
            middle
            - (moved(up1, j, 1, lane) + moved(down1, j, -1, lane))
            - (moved(up2, j, 2, lane) + moved(down2, j, -2, lane))
        )
        yield j, lap * lap


def gather_sum(tiles, sub):
    low = sub < 4
    tiles = [
        jnp.where(low, a, b) + pltpu.roll(jnp.where(low, b, a), 4, axis=0) for a, b in zip(tiles[:4], tiles[4:])
    ]
    for d in (2, 1):
        pick = (sub & d) == 0
        tiles = [
            jnp.where(pick, a + pltpu.roll(a, 8 - d, axis=0), b + pltpu.roll(b, d, axis=0))
            for a, b in zip(tiles[:d], tiles[d:])
        ]
    return tiles[0]


def partials_row(energy, cell, store, count, lane, sub):
    cols = [((energy(0, j) + energy(1, j)) + (energy(3, j) + energy(4, j))) + energy(2, j) for j in range(count)]
    turned = {step: rotated(cols, step) for step in (1, -1, 2, -2)}
    for block in range(0, count, 8):
        tops, totals, blends = None, [], []
        for j in range(block, block + 8):
            box = cols[j] + ((moved(turned[1], j, 1, lane) + moved(turned[-1], j, -1, lane)) + (
                moved(turned[2], j, 2, lane) + moved(turned[-2], j, -2, lane)))
            score = box * (sharpness * log2e)
            top = jnp.max(score, axis=0, keepdims=True)
            weight = jnp.exp2(score - top)
            blend = weight * cell(j)
            totals.append(weight[0:8] + weight[8:16])
            blends.append(blend[0:8] + blend[8:16])
            tall = jnp.broadcast_to(top, (8, LANES))
            tops = tall if tops is None else jnp.where(sub == j - block, tall, tops)
        total = gather_sum(totals, sub)
        store(0, block, tops + jnp.log2(total))
        store(1, block, gather_sum(blends, sub) / total)


def grid_of(rows, cols):
    return lax.broadcasted_iota(jnp.int32, (rows, cols), 0), lax.broadcasted_iota(jnp.int32, (rows, cols), 1)


def lanes_and_subs(planes):
    return (
        lax.broadcasted_iota(jnp.int32, (planes, LANES), 1),
        lax.broadcasted_iota(jnp.int32, (8, LANES), 0),
    )


def turn_kernel(x_ref, xt_ref, a_ref, b_ref, *, chunk):
    planes, rows, cols = x_ref.shape
    n = planes * rows
    o, k = grid_of(n, n)
    swap = jnp.where((o // planes == k % rows) & (o % planes == k // rows), 1.0, 0.0).astype(jnp.bfloat16)
    for c in range(cols // chunk):
        ds = pl.ds(c * chunk, chunk)
        y = jnp.dot(swap, x_ref[:, :, ds].reshape(n, chunk), preferred_element_type=jnp.float32)
        xt_ref[:, :, ds] = y.reshape(rows, planes, chunk)
    odd = lax.rem(lax.axis_index("xy"), 2)
    last = rows - HALO
    a_ref[...] = xt_ref[pl.ds(last - odd * last, HALO)].astype(jnp.bfloat16)
    b_ref[...] = xt_ref[pl.ds(odd * last, HALO)].astype(jnp.bfloat16)


def inner_kernel(xt_ref, energy_ref, part_ref):
    rows, planes, cols = xt_ref.shape
    count = cols // LANES
    lane, sub = lanes_and_subs(planes)

    def first(r, carry):
        for j, value in energy_row(lambda k, j: xt_ref[r + k, :, tile(j)], count, lane):
            energy_ref[r, :, tile(j)] = value
        return carry

    lax.fori_loop(0, rows - 4, first, 0, unroll=UNROLL)

    def second(r, carry):
        def store(q, block, value):
            part_ref[q, r, block:block + 8, :] = value

        partials_row(
            lambda k, j: energy_ref[r + k, :, tile(j)], lambda j: xt_ref[r + 4, :, tile(j)], store, count, lane, sub
        )
        return carry

    lax.fori_loop(0, rows - 8, second, 0, unroll=UNROLL)


def side_rows(below, xt_ref, got_ref, energy_ref, part, cells, energy):
    rows, planes, cols = xt_ref.shape
    count = cols // LANES
    lane, sub = lanes_and_subs(planes)
    me = lax.axis_index("xy")
    at_end = me == jnp.where(below == 1, lax.axis_size("xy") - 1, 0)
    flip = 3 * below
    for i in range(HALO):
        cells[i] = got_ref[i ^ flip].astype(jnp.float32)
        cells[HALO + i] = xt_ref[(rows - HALO) * below + (i ^ flip)]
        energy[HALO + i] = energy_ref[(rows - 8) * below + (i ^ flip)]

    def first(i, carry):
        keep = jnp.where((i < 2) & at_end, 0.0, 1.0)
        for j, value in energy_row(lambda k, j: cells[i + k, :, tile(j)], count, lane):
            energy[i, :, tile(j)] = value * keep
        return carry

    lax.fori_loop(0, HALO, first, 0, unroll=UNROLL)

    def second(i, carry):
        def store(q, block, value):
            part[q, HALO * below + (i ^ flip), block:block + 8, :] = value

        partials_row(
            lambda k, j: energy[i + k, :, tile(j)], lambda j: cells[HALO + i, :, tile(j)], store, count, lane, sub
        )
        return carry

    lax.fori_loop(0, HALO, second, 0, unroll=UNROLL)


def near_kernel(xt_ref, got_ref, energy_ref, part_ref, cells, energy):
    below = 1 - lax.rem(lax.axis_index("xy"), 2)
    side_rows(below, xt_ref, got_ref, energy_ref, part_ref, cells, energy)


def far_kernel(xt_ref, got_ref, energy_ref, inner_ref, near_ref, out_ref, cells, energy, part):
    rows, _, cols = xt_ref.shape
    count = cols // LANES
    below = lax.rem(lax.axis_index("xy"), 2)
    side_rows(below, xt_ref, got_ref, energy_ref, part, cells, energy)
    for q in range(2):
        for i in range(HALO):
            slot = HALO * (1 - below) + i
            part[q, slot] = near_ref[q, slot]
    each = count // out_ref.shape[0]
    for q in range(2):
        for h, ref in enumerate((inner_ref, part)):
            for j in range(count):
                flat = ref.at[q].reshape(8 * count, LANES)
                out_ref[j // each, q * rows + 8 * h:q * rows + 8 * h + 8, tile(j % each)] = (
                    flat[pl.ds(j, 8, stride=count), :]
                )


def join_kernel(in_ref, joined_ref, pooled_ref, half):
    groups, twice, own = in_ref.shape
    rows = twice // 2
    logs = [in_ref[g, 0:rows, :] for g in range(groups)]
    top = functools.reduce(jnp.maximum, logs)
    weights = [jnp.exp2(v - top) for v in logs]
    total = functools.reduce(jnp.add, weights)
    blend = functools.reduce(jnp.add, [w * in_ref[g, rows:twice, :] for g, w in enumerate(weights)])
    joined = blend / total
    joined_ref[HALO:HALO + 8, :] = joined[0:8]
    joined_ref[0:HALO, :] = joined[8:12]
    joined_ref[HALO + 8:rows, :] = joined[12:16]
    halves = []
    for h in range(own // LANES):
        half[h] = joined_ref[:, tile(h)]
        even, uneven = (half.at[h][pl.ds(k, rows // 2, stride=2), :] for k in range(2))
        halves.append(even + uneven)
    halves = jnp.concatenate(halves, axis=1)
    r, c = grid_of(own, own // 2)
    col_pairs = jnp.where(r // 2 == c, 0.25, 0.0)
    pooled_ref[...] = jnp.dot(
        halves, col_pairs, preferred_element_type=jnp.float32, precision=lax.Precision.HIGHEST
    )


def vmem(count):
    return [pl.BlockSpec(memory_space=pltpu.VMEM)] * count


def params(mib):
    return pltpu.CompilerParams(vmem_limit_bytes=mib << 20)


def cost(flops):
    return pl.CostEstimate(flops=flops, bytes_accessed=4 << 20, transcendentals=10**6)


def shards(stack):
    planes, rows, cols = stack.shape
    f32, bf16 = jnp.float32, jnp.bfloat16
    sds = jax.ShapeDtypeStruct
    strip = sds((HALO, planes, cols), bf16)
    count = cols // LANES
    xt, to_a, to_b = pl.pallas_call(
        functools.partial(turn_kernel, chunk=512),
        out_shape=(sds((rows, planes, cols), f32), strip, strip),
        in_specs=vmem(1),
        out_specs=tuple(vmem(3)),
        compiler_params=params(8),
        cost_estimate=cost(10**7),
        name="turn",
    )(stack)
    devices = lax.axis_size("xy")
    ends = [(i, i + 1) for i in range(1, devices - 1, 2)]
    from_b = lax.ppermute(to_b, "xy", ends + [(j, i) for i, j in ends])
    from_a = lax.ppermute(to_a, "xy", [(i, i ^ 1) for i in range(devices)])
    energy, inner = pl.pallas_call(
        inner_kernel,
        out_shape=(sds((rows - 4, planes, cols), f32), sds((2, rows - 8, count, LANES), f32)),
        in_specs=vmem(1),
        out_specs=tuple(vmem(2)),
        compiler_params=params(8),
        cost_estimate=cost(10**8),
        name="inner",
    )(xt)
    side_scratch = [pltpu.VMEM((2 * HALO, planes, cols), f32)] * 2
    part = sds((2, 2 * HALO, count, LANES), f32)
    near = pl.pallas_call(
        near_kernel,
        out_shape=part,
        in_specs=vmem(3),
        out_specs=vmem(1)[0],
        scratch_shapes=side_scratch,
        compiler_params=params(8),
        cost_estimate=cost(10**8),
        name="near",
    )(xt, from_a, energy)
    groups = lax.axis_size("gz")
    own = cols // groups
    ready = pl.pallas_call(
        far_kernel,
        out_shape=sds((groups, 2 * rows, own), f32),
        in_specs=vmem(5),
        out_specs=vmem(1)[0],
        scratch_shapes=side_scratch + [pltpu.VMEM(part.shape, f32)],
        compiler_params=params(8),
        cost_estimate=cost(10**8),
        name="far",
    )(xt, from_b, energy, inner, near)
    parts = lax.all_to_all(ready, "gz", split_axis=0, concat_axis=0, tiled=True)
    return pl.pallas_call(
        join_kernel,
        out_shape=(sds((rows, own), f32), sds((rows // 2, own // 2), f32)),
        in_specs=vmem(1),
        out_specs=tuple(vmem(2)),
        scratch_shapes=[pltpu.VMEM((own // LANES, rows, LANES), f32)],
        compiler_params=params(4),
        name="join",
    )(parts)


def solution(mesh):
    in_specs = (P("gz", "xy", None),)
    out_specs = (P("xy", "gz"), P("xy", "gz"))
    return jax.shard_map(shards, mesh=mesh, in_specs=in_specs, out_specs=out_specs, check_vma=False)
```

time: 39.4 us -> 38 us (0.964)
  waiting for transfers between devices: 1.46 us -> 0.03 us
  Pallas kernels: 8.96 us -> 8.55 us
  blocking collectives: 22.5 us -> 22.9 us
    ppermute x1, waiting for transfers between devices: 1.46 us -> 0.02 us  [shards(): from_b = lax.ppermute(to_b, 'xy', ends + [(j, i) for i, j in ends])]
    all_to_all x1, blocking collectives: 22.5 us -> 22.9 us  [shards(): parts = lax.all_to_all(ready, 'gz', split_axis=0, concat_axis=0, tiled=True)]
    pallas_call x2 -> x3, Pallas kernels: 7.47 us -> 7.15 us  [the longest x1 3.78 us: shards(): pl.pallas_call(inner_kernel, out_shape=(sds((rows - 4, planes, cols), f32...]
  transfers between devices with their start and end apart: 2 -> 2, of which waited for: 1 -> 0; matrix products, arithmetic and copies ran while one was open for 0% -> 0% of each run, Pallas kernels for 10% -> 14%
where the time goes in v2:
time: 38 us; the launch traced here: 37.8 us
  blocking collectives  22.9 us (60%)
  Pallas kernels  8.55 us (23%)
  starting transfers between devices  4.41 us (12%)
  local copies, waits for them, and re-layouts  1.22 us (3%)
  between operations  0.69 us (2%)
    all_to_all x1, blocking collectives, shards(): parts = lax.all_to_all(ready, 'gz', split_axis=0, concat_axis=0, tiled=True)  22.9 us
    ppermute x1, starting transfers between devices, shards(): from_b = lax.ppermute(to_b, 'xy', ends + [(j, i) for i, j in ends])  4.31 us
    pallas_call x1, Pallas kernels, shards(): pl.pallas_call(inner_kernel, out_shape=(sds((rows - 4, planes, cols), f32...  3.78 us
    pallas_call x1, Pallas kernels, shards(): pl.pallas_call(far_kernel, out_shape=sds((groups, 2 * rows, own), f32), i...  1.72 us
    pallas_call x1, Pallas kernels, shards(): pl.pallas_call(near_kernel, out_shape=part, in_specs=vmem(3), out_specs=v...  1.65 us
    unnamed x2, local copies, waits for them, and re-layouts  1.22 us
    pallas_call x1, Pallas kernels, shards(): pl.pallas_call(join_kernel, out_shape=(sds((rows, own), f32), sds((rows /...  0.84 us
  transfers between devices with their start and end apart: 2, of which 0 were waited for; matrix products, arithmetic and copies ran while one was open for 0% of the time, Pallas kernels for 14%

profile of v2, /device:TPU:32, one launch (start us, length us, event | category | flops | bytes accessed | tf_op | source)
XLA Modules:
  0.0 37.8 jit_solution(16124257108751398425)
XLA Ops:
  0.6 0.0 copy-start
  0.6 1.2 %copy-done = bf16[16,16,2048]{2,1,0:T(8,128)(2,1)S(1)} copy-done((bf16[16,16,2048]{2,1,0:T(8,128)(2,1)S(1)}, bf16[16,16,2048]{2,1,0:T(8,128)(2,1)}, u32[]{:S(2)}) %copy-start) | copy-done | bytes 1048600
  1.9 0.6 %turn.1 = (f32[16,16,2048]{2,1,0:T(8,128)S(1)}, bf16[4,16,2048]{2,1,0:T(8,128)(2,1)S(1)}, bf16[4,16,2048]{2,1,0:T(8,128)(2,1)S(1)}) custom-call(bf16[16,16,2048]{2,1,0:T(8,128)(2,1)S(1)} %copy-done), custom_call_target="tpu_custom_call" | custom-call | flops 10000000 | bytes 4194304 | tf_op jit(solution)/shard_map/turn/pallas_call | solution.py:233
  2.4 0.1 collective-permute-start.1
  2.5 4.3 %collective-permute-start = (bf16[4,16,2048]{2,1,0:T(8,128)(2,1)S(1)}, bf16[4,16,2048]{2,1,0:T(8,128)(2,1)S(1)}, u32[]{:S(2)}, u32[]{:S(2)}) collective-permute-start(bf16[4,16,2048]{2,1,0:T(8,128)(2,1)S(1)} %get-tuple-element.8), channel_id=1, source_target_pairs={{1,2},{3,4},{5,6},{7,8},{9,10},{11,12},{13,14},{15,16},{17,18},{19... | collective-permute-start | bytes 786440 | tf_op jit(solution)/shard_map/ppermute | solution.py:244
  6.8 3.8 %inner.1 = (f32[12,16,2048]{2,1,0:T(8,128)S(1)}, f32[2,8,16,128]{3,2,1,0:T(8,128)S(1)}) custom-call(f32[16,16,2048]{2,1,0:T(8,128)S(1)} %get-tuple-element.7.xt_ref), custom_call_target="tpu_custom_call" | custom-call | flops 100000000 | bytes 4194304 | tf_op jit(solution)/shard_map/inner/pallas_call | solution.py:246
  10.6 0.0 collective-permute-done.1.got_ref
  10.6 1.7 %near.1.near_ref = f32[2,8,16,128]{3,2,1,0:T(8,128)S(1)} custom-call(f32[16,16,2048]{2,1,0:T(8,128)S(1)} %get-tuple-element.7.xt_ref, bf16[4,16,2048]{2,1,0:T(8,128)(2,1)S(1)} %collective-permute-done.1.got_ref, f32[12,16,2048]{2,1,0:T(8,128)S(1)} %get-tuple-element.9.energy_ref), custom_call_target="tpu_custom_call" | custom-call | flops 100000000 | bytes 4194304 | tf_op jit(solution)/shard_map/near/pallas_call | solution.py:257
  12.3 0.0 collective-permute-done.got_ref
  12.3 1.7 %far.1 = f32[8,32,256]{2,1,0:T(8,128)S(1)} custom-call(f32[16,16,2048]{2,1,0:T(8,128)S(1)} %get-tuple-element.7.xt_ref, bf16[4,16,2048]{2,1,0:T(8,128)(2,1)S(1)} %collective-permute-done.got_ref, f32[12,16,2048]{2,1,0:T(8,128)S(1)} %get-tuple-element.9.energy_ref, f32[2,8,16,128]{3,2,1,0:T(8,128)S(1)} %get-tuple-element.10.inner_ref, ...), custom_call_target="tpu_custom_call" | custom-call | flops 100000000 | bytes 4194304 | tf_op jit(solution)/shard_map/far/pallas_call | solution.py:269
  14.0 22.9 %all_to_all.5.in_ref = f32[8,32,256]{2,1,0:T(8,128)S(1)} all-to-all(f32[8,32,256]{2,1,0:T(8,128)S(1)} %far.1), channel_id=1, replica_groups=mesh['gz'=8,'xy'=32] {'gz'}, dimensions={0} | all-to-all | bytes 524288 | tf_op jit(solution)/shard_map/all_to_all | solution.py:279
  37.0 0.8 %join.1 = (f32[16,256]{1,0:T(8,128)}, f32[8,128]{1,0:T(8,128)}) custom-call(f32[8,32,256]{2,1,0:T(8,128)S(1)} %all_to_all.5.in_ref), custom_call_target="tpu_custom_call" | custom-call | tf_op jit(solution)/shard_map/join/pallas_call | solution.py:280
Async XLA Ops:
  0.6 1.2 %copy-start = (bf16[16,16,2048]{2,1,0:T(8,128)(2,1)S(1)}, bf16[16,16,2048]{2,1,0:T(8,128)(2,1)}, u32[]{:S(2)}) copy-start(bf16[16,16,2048]{2,1,0:T(8,128)(2,1)} %x_ref.1) | copy-start | bytes 3145732
  2.4 8.2 %collective-permute-start.1 = (bf16[4,16,2048]{2,1,0:T(8,128)(2,1)S(1)}, bf16[4,16,2048]{2,1,0:T(8,128)(2,1)S(1)}, u32[]{:S(2)}, u32[]{:S(2)}) collective-permute-start(bf16[4,16,2048]{2,1,0:T(8,128)(2,1)S(1)} %get-tuple-element.11), channel_id=1, source_target_pairs={{0,1},{1,0},{2,3},{3,2},{4,5},{5,4},{6,7},{7,6},{8,9},{9,8},{10,11... | collective-permute-start | bytes 786440 | tf_op jit(solution)/shard_map/ppermute | solution.py:245
  2.5 9.8 %collective-permute-start = (bf16[4,16,2048]{2,1,0:T(8,128)(2,1)S(1)}, bf16[4,16,2048]{2,1,0:T(8,128)(2,1)S(1)}, u32[]{:S(2)}, u32[]{:S(2)}) collective-permute-start(bf16[4,16,2048]{2,1,0:T(8,128)(2,1)S(1)} %get-tuple-element.8), channel_id=1, source_target_pairs={{1,2},{3,4},{5,6},{7,8},{9,10},{11,12},{13,14},{15,16},{17,18},{19... | collective-permute-start | bytes 786440 | tf_op jit(solution)/shard_map/ppermute | solution.py:244

commit v3 on v2

--- a/solution.py
+++ b/solution.py
@@ -13,6 +13,7 @@
 LANES = 128
 HALO = 4
 UNROLL = 2
+UNROLL2 = 1
 
 
 def tile(j):
@@ -60,25 +61,41 @@
     return tiles[0]
 
 
-def partials_row(energy, cell, store, count, lane, sub):
-    cols = [((energy(0, j) + energy(1, j)) + (energy(3, j) + energy(4, j))) + energy(2, j) for j in range(count)]
-    turned = {step: rotated(cols, step) for step in (1, -1, 2, -2)}
-    for block in range(0, count, 8):
+def box_of(cols, lane):
+    count = len(cols)
+    left = rotated(cols, -1)
+    pairs = [c + moved(left, j, -1, lane) for j, c in enumerate(cols)]
+    right = rotated(pairs, 2)
+    after = jnp.where(lane == LANES - 2, pltpu.roll(cols[-1], LANES - 1, axis=1), 0.0)
+    far = rotated(cols, -2)
+    for j in range(count):
+        other = right[j + 1] if j + 1 < count else after
+        fours = pairs[j] + jnp.where(lane < LANES - 2, right[j], other)
+        yield fours + moved(far, j, -2, lane)
+
+
+def partials_rows(energy, cell, store, count, lane, sub):
+    both = ([], [])
+    for j in range(count):
+        shared = (energy(1, j) + energy(2, j)) + (energy(3, j) + energy(4, j))
+        both[0].append(shared + energy(0, j))
+        both[1].append(shared + energy(5, j))
+    for row, cols in enumerate(both):
         tops, totals, blends = None, [], []
-        for j in range(block, block + 8):
-            box = cols[j] + ((moved(turned[1], j, 1, lane) + moved(turned[-1], j, -1, lane)) + (
-                moved(turned[2], j, 2, lane) + moved(turned[-2], j, -2, lane)))
+        for j, box in enumerate(box_of(cols, lane)):
             score = box * (sharpness * log2e)
             top = jnp.max(score, axis=0, keepdims=True)
             weight = jnp.exp2(score - top)
-            blend = weight * cell(j)
+            blend = weight * cell(row, j)
             totals.append(weight[0:8] + weight[8:16])
             blends.append(blend[0:8] + blend[8:16])
             tall = jnp.broadcast_to(top, (8, LANES))
-            tops = tall if tops is None else jnp.where(sub == j - block, tall, tops)
-        total = gather_sum(totals, sub)
-        store(0, block, tops + jnp.log2(total))
-        store(1, block, gather_sum(blends, sub) / total)
+            tops = tall if tops is None else jnp.where(sub == j % 8, tall, tops)
+            if j % 8 == 7:
+                total = gather_sum(totals, sub)
+                store(0, row, j - 7, tops + jnp.log2(total))
+                store(1, row, j - 7, gather_sum(blends, sub) / total)
+                tops, totals, blends = None, [], []
 
 
 def grid_of(rows, cols):
@@ -119,16 +136,20 @@
 
     lax.fori_loop(0, rows - 4, first, 0, unroll=UNROLL)
 
-    def second(r, carry):
-        def store(q, block, value):
-            part_ref[q, r, block:block + 8, :] = value
-
-        partials_row(
-            lambda k, j: energy_ref[r + k, :, tile(j)], lambda j: xt_ref[r + 4, :, tile(j)], store, count, lane, sub
+    def second(h, carry):
+        r = 2 * h
+
+        def store(q, row, block, value):
+            part_ref[q, r + row, block:block + 8, :] = value
+
+        partials_rows(
+            lambda k, j: energy_ref[r + k, :, tile(j)],
+            lambda row, j: xt_ref[r + row + 4, :, tile(j)],
+            store, count, lane, sub,
         )
         return carry
 
-    lax.fori_loop(0, rows - 8, second, 0, unroll=UNROLL)
+    lax.fori_loop(0, (rows - 8) // 2, second, 0, unroll=UNROLL2)
 
 
 def side_rows(below, xt_ref, got_ref, energy_ref, part, cells, energy):
@@ -151,16 +172,20 @@
 
     lax.fori_loop(0, HALO, first, 0, unroll=UNROLL)
 
-    def second(i, carry):
-        def store(q, block, value):
-            part[q, HALO * below + (i ^ flip), block:block + 8, :] = value
-
-        partials_row(
-            lambda k, j: energy[i + k, :, tile(j)], lambda j: cells[HALO + i, :, tile(j)], store, count, lane, sub
+    def second(h, carry):
+        i = 2 * h
+
+        def store(q, row, block, value):
+            part[q, HALO * below + ((i + row) ^ flip), block:block + 8, :] = value
+
+        partials_rows(
+            lambda k, j: energy[i + k, :, tile(j)],
+            lambda row, j: cells[HALO + i + row, :, tile(j)],
+            store, count, lane, sub,
         )
         return carry
 
-    lax.fori_loop(0, HALO, second, 0, unroll=UNROLL)
+    lax.fori_loop(0, HALO // 2, second, 0, unroll=UNROLL2)
 
 
 def near_kernel(xt_ref, got_ref, energy_ref, part_ref, cells, energy):
@@ -177,25 +202,39 @@
         for i in range(HALO):
             slot = HALO * (1 - below) + i
             part[q, slot] = near_ref[q, slot]
-    each = count // out_ref.shape[0]
+    inner_groups, outer_groups = out_ref.shape[:2]
+    each = count // (inner_groups * outer_groups)
     for q in range(2):
         for h, ref in enumerate((inner_ref, part)):
             for j in range(count):
                 flat = ref.at[q].reshape(8 * count, LANES)
-                out_ref[j // each, q * rows + 8 * h:q * rows + 8 * h + 8, tile(j % each)] = (
-                    flat[pl.ds(j, 8, stride=count), :]
-                )
-
-
-def join_kernel(in_ref, joined_ref, pooled_ref, half):
-    groups, twice, own = in_ref.shape
+                owner = j // each
+                out_ref[owner % inner_groups, owner // inner_groups, q * rows + 8 * h:q * rows + 8 * h + 8,
+                        tile(j % each)] = flat[pl.ds(j, 8, stride=count), :]
+
+
+def merged(entries):
+    top = functools.reduce(jnp.maximum, [v for v, _ in entries])
+    weights = [jnp.exp2(v - top) for v, _ in entries]
+    total = functools.reduce(jnp.add, weights)
+    blend = functools.reduce(jnp.add, [w * mean for w, (_, mean) in zip(weights, entries)])
+    return top, total, blend / total
+
+
+def merge_kernel(in_ref, out_ref, *, other):
+    inner_groups, _, twice, _ = in_ref.shape
     rows = twice // 2
-    logs = [in_ref[g, 0:rows, :] for g in range(groups)]
-    top = functools.reduce(jnp.maximum, logs)
-    weights = [jnp.exp2(v - top) for v in logs]
-    total = functools.reduce(jnp.add, weights)
-    blend = functools.reduce(jnp.add, [w * in_ref[g, rows:twice, :] for g, w in enumerate(weights)])
-    joined = blend / total
+    mine = lax.axis_index("gz") // inner_groups
+    block = 1 - mine if other else mine
+    top, total, mean = merged([(in_ref[g, block, 0:rows, :], in_ref[g, block, rows:, :]) for g in range(inner_groups)])
+    out_ref[0:rows, :] = top + jnp.log2(total)
+    out_ref[rows:, :] = mean
+
+
+def join_kernel(kept_ref, got_ref, joined_ref, pooled_ref, half):
+    twice, own = kept_ref.shape
+    rows = twice // 2
+    _, _, joined = merged([(ref[0:rows, :], ref[rows:, :]) for ref in (kept_ref, got_ref)])
     joined_ref[HALO:HALO + 8, :] = joined[0:8]
     joined_ref[0:HALO, :] = joined[8:12]
     joined_ref[HALO + 8:rows, :] = joined[12:16]
@@ -266,9 +305,11 @@
     )(xt, from_a, energy)
     groups = lax.axis_size("gz")
     own = cols // groups
+    outer_groups = 2
+    inner_groups = groups // outer_groups
     ready = pl.pallas_call(
         far_kernel,
-        out_shape=sds((groups, 2 * rows, own), f32),
+        out_shape=sds((inner_groups, outer_groups, 2 * rows, own), f32),
         in_specs=vmem(5),
         out_specs=vmem(1)[0],
         scratch_shapes=side_scratch + [pltpu.VMEM(part.shape, f32)],
@@ -276,16 +317,32 @@
         cost_estimate=cost(10**8),
         name="far",
     )(xt, from_b, energy, inner, near)
-    parts = lax.all_to_all(ready, "gz", split_axis=0, concat_axis=0, tiled=True)
+    teams = [[o * inner_groups + i for i in range(inner_groups)] for o in range(outer_groups)]
+    parts = lax.all_to_all(ready, "gz", split_axis=0, concat_axis=0, tiled=True, axis_index_groups=teams)
+
+    def merge(other):
+        return pl.pallas_call(
+            functools.partial(merge_kernel, other=other),
+            out_shape=sds((2 * rows, own), f32),
+            in_specs=vmem(1),
+            out_specs=vmem(1)[0],
+            compiler_params=params(4),
+            cost_estimate=cost(10**6),
+            name="merge_other" if other else "merge_own",
+        )(parts)
+
+    leaving = merge(True)
+    got = lax.ppermute(leaving, "gz", [(i, (i + inner_groups) % groups) for i in range(groups)])
+    kept = merge(False)
     return pl.pallas_call(
         join_kernel,
         out_shape=(sds((rows, own), f32), sds((rows // 2, own // 2), f32)),
-        in_specs=vmem(1),
+        in_specs=vmem(2),
         out_specs=tuple(vmem(2)),
         scratch_shapes=[pltpu.VMEM((own // LANES, rows, LANES), f32)],
         compiler_params=params(4),
         name="join",
-    )(parts)
+    )(kept, got)
 
 
 def solution(mesh):

time: 38 us -> 35.2 us (0.926)
  blocking collectives: 22.9 us -> 10.9 us
  starting transfers between devices: 4.41 us -> 11.7 us
  waiting for transfers between devices: 0.03 us -> 1.88 us
    all_to_all x1, blocking collectives: 22.9 us -> 10.9 us  [shards(): lax.all_to_all(ready, 'gz', split_axis=0, concat_axis=0, tiled=True, axis...]
    ppermute x0 -> x1, starting transfers between devices: none -> 7.27 us  [shards(): lax.ppermute(leaving, 'gz', [(i, (i + inner_groups) % groups) for i in ra...]
    ppermute x0 -> x1, waiting for transfers between devices: none -> 1.86 us  [shards(): lax.ppermute(leaving, 'gz', [(i, (i + inner_groups) % groups) for i in ra...]
    pallas_call x1 -> x3, Pallas kernels: 1.72 us -> 1.78 us  [the longest x1 1.72 us: shards(): pl.pallas_call(far_kernel, out_shape=sds((inner_groups, outer_groups, 2 *...]
  transfers between devices with their start and end apart: 2 -> 3, of which waited for: 0 -> 1; matrix products, arithmetic and copies ran while one was open for 0% -> 0% of each run, Pallas kernels for 14% -> 16%
where the time goes in v3:
time: 35.2 us; the launch traced here: 35 us
  starting transfers between devices  11.7 us (33%)
  blocking collectives  10.9 us (31%)
  Pallas kernels  8.6 us (24%)
  waiting for transfers between devices  1.88 us (5%)
  local copies, waits for them, and re-layouts  1.22 us (3%)
  between operations  0.7 us (2%)
    all_to_all x1, blocking collectives, shards(): lax.all_to_all(ready, 'gz', split_axis=0, concat_axis=0, tiled=True, axis...  10.9 us
    ppermute x1, starting transfers between devices, shards(): lax.ppermute(leaving, 'gz', [(i, (i + inner_groups) % groups) for i in ra...  7.27 us
    ppermute x1, starting transfers between devices, shards(): from_b = lax.ppermute(to_b, 'xy', ends + [(j, i) for i, j in ends])  4.31 us
    pallas_call x1, Pallas kernels, shards(): pl.pallas_call(inner_kernel, out_shape=(sds((rows - 4, planes, cols), f32...  3.78 us
    ppermute x1, waiting for transfers between devices, shards(): lax.ppermute(leaving, 'gz', [(i, (i + inner_groups) % groups) for i in ra...  1.86 us
    pallas_call x1, Pallas kernels, shards(): pl.pallas_call(far_kernel, out_shape=sds((inner_groups, outer_groups, 2 *...  1.72 us
    pallas_call x1, Pallas kernels, shards(): pl.pallas_call(near_kernel, out_shape=part, in_specs=vmem(3), out_specs=v...  1.65 us
    unnamed x2, local copies, waits for them, and re-layouts  1.22 us
  transfers between devices with their start and end apart: 3, of which 1 were waited for; matrix products, arithmetic and copies ran while one was open for 0% of the time, Pallas kernels for 16%

profile of v3, /device:TPU:32, one launch (start us, length us, event | category | flops | bytes accessed | tf_op | source)
XLA Modules:
  0.0 35.0 jit_solution(13512305711714512339)
XLA Ops:
  0.6 0.0 copy-start
  0.6 1.2 %copy-done = bf16[16,16,2048]{2,1,0:T(8,128)(2,1)S(1)} copy-done((bf16[16,16,2048]{2,1,0:T(8,128)(2,1)S(1)}, bf16[16,16,2048]{2,1,0:T(8,128)(2,1)}, u32[]{:S(2)}) %copy-start) | copy-done | bytes 1048600
  1.9 0.6 %turn.1 = (f32[16,16,2048]{2,1,0:T(8,128)S(1)}, bf16[4,16,2048]{2,1,0:T(8,128)(2,1)S(1)}, bf16[4,16,2048]{2,1,0:T(8,128)(2,1)S(1)}) custom-call(bf16[16,16,2048]{2,1,0:T(8,128)(2,1)S(1)} %copy-done), custom_call_target="tpu_custom_call" | custom-call | flops 10000000 | bytes 4194304 | tf_op jit(solution)/shard_map/turn/pallas_call | solution.py:272
  2.4 0.1 collective-permute-start.1
  2.5 4.3 %collective-permute-start = (bf16[4,16,2048]{2,1,0:T(8,128)(2,1)S(1)}, bf16[4,16,2048]{2,1,0:T(8,128)(2,1)S(1)}, u32[]{:S(2)}, u32[]{:S(2)}) collective-permute-start(bf16[4,16,2048]{2,1,0:T(8,128)(2,1)S(1)} %get-tuple-element.8), channel_id=1, source_target_pairs={{1,2},{3,4},{5,6},{7,8},{9,10},{11,12},{13,14},{15,16},{17,18},{19... | collective-permute-start | bytes 786440 | tf_op jit(solution)/shard_map/ppermute | solution.py:283
  6.8 3.8 %inner.1 = (f32[12,16,2048]{2,1,0:T(8,128)S(1)}, f32[2,8,16,128]{3,2,1,0:T(8,128)S(1)}) custom-call(f32[16,16,2048]{2,1,0:T(8,128)S(1)} %get-tuple-element.7.xt_ref), custom_call_target="tpu_custom_call" | custom-call | flops 100000000 | bytes 4194304 | tf_op jit(solution)/shard_map/inner/pallas_call | solution.py:285
  10.6 0.0 collective-permute-done.1.got_ref
  10.6 1.7 %near.1.near_ref = f32[2,8,16,128]{3,2,1,0:T(8,128)S(1)} custom-call(f32[16,16,2048]{2,1,0:T(8,128)S(1)} %get-tuple-element.7.xt_ref, bf16[4,16,2048]{2,1,0:T(8,128)(2,1)S(1)} %collective-permute-done.1.got_ref, f32[12,16,2048]{2,1,0:T(8,128)S(1)} %get-tuple-element.9.energy_ref), custom_call_target="tpu_custom_call" | custom-call | flops 100000000 | bytes 4194304 | tf_op jit(solution)/shard_map/near/pallas_call | solution.py:296
  12.3 0.0 collective-permute-done.got_ref
  12.3 1.7 %far.1 = f32[4,2,32,256]{3,2,1,0:T(8,128)S(1)} custom-call(f32[16,16,2048]{2,1,0:T(8,128)S(1)} %get-tuple-element.7.xt_ref, bf16[4,16,2048]{2,1,0:T(8,128)(2,1)S(1)} %collective-permute-done.got_ref, f32[12,16,2048]{2,1,0:T(8,128)S(1)} %get-tuple-element.9.energy_ref, f32[2,8,16,128]{3,2,1,0:T(8,128)S(1)} %get-tuple-element.10.inner_ref, ...), custom_call_target="tpu_custom_call" | custom-call | flops 100000000 | bytes 4194304 | tf_op jit(solution)/shard_map/far/pallas_call | solution.py:310
  14.1 10.9 %all_to_all.5.in_ref = f32[4,2,32,256]{3,2,1,0:T(8,128)S(1)} all-to-all(f32[4,2,32,256]{3,2,1,0:T(8,128)S(1)} %far.1), channel_id=1, replica_groups={{0,32,64,96},{128,160,192,224},{1,33,65,97},{129,161,193,225},{2,34,66,..., dimensions={0} | all-to-all | bytes 524288 | tf_op jit(solution)/shard_map/all_to_all | solution.py:321
  25.0 7.3 %collective-permute-start.2 = (f32[32,256]{1,0:T(8,128)S(1)}, f32[32,256]{1,0:T(8,128)S(1)}, u32[]{:S(2)}, u32[]{:S(2)}) collective-permute-start(f32[32,256]{1,0:T(8,128)S(1)} %merge_other.1), channel_id=1, source_target_pairs={{0,128},{32,160},{64,192},{96,224},{128,0},{160,32},{192,64},{224,... | collective-permute-start | bytes 98312 | tf_op jit(solution)/shard_map/ppermute | solution.py:335
  32.3 1.9 %collective-permute-done.2.got_ref = f32[32,256]{1,0:T(8,128)S(1)} collective-permute-done((f32[32,256]{1,0:T(8,128)S(1)}, f32[32,256]{1,0:T(8,128)S(1)}, u32[]{:S(2)}, u32[]{:S(2)}) %collective-permute-start.2) | collective-permute-done | bytes 32800 | tf_op jit(solution)/shard_map/ppermute | solution.py:335
  34.2 0.8 %join.1 = (f32[16,256]{1,0:T(8,128)}, f32[8,128]{1,0:T(8,128)}) custom-call(f32[32,256]{1,0:T(8,128)S(1)} %merge_own.1.kept_ref, f32[32,256]{1,0:T(8,128)S(1)} %collective-permute-done.2.got_ref), custom_call_target="tpu_custom_call" | custom-call | tf_op jit(solution)/shard_map/join/pallas_call | solution.py:337
  (2 shorter events, 0.1 us)
Async XLA Ops:
  0.6 1.2 %copy-start = (bf16[16,16,2048]{2,1,0:T(8,128)(2,1)S(1)}, bf16[16,16,2048]{2,1,0:T(8,128)(2,1)}, u32[]{:S(2)}) copy-start(bf16[16,16,2048]{2,1,0:T(8,128)(2,1)} %x_ref.1) | copy-start | bytes 3145732
  2.4 8.2 %collective-permute-start.1 = (bf16[4,16,2048]{2,1,0:T(8,128)(2,1)S(1)}, bf16[4,16,2048]{2,1,0:T(8,128)(2,1)S(1)}, u32[]{:S(2)}, u32[]{:S(2)}) collective-permute-start(bf16[4,16,2048]{2,1,0:T(8,128)(2,1)S(1)} %get-tuple-element.11), channel_id=1, source_target_pairs={{0,1},{1,0},{2,3},{3,2},{4,5},{5,4},{6,7},{7,6},{8,9},{9,8},{10,11... | collective-permute-start | bytes 786440 | tf_op jit(solution)/shard_map/ppermute | solution.py:284
  2.5 9.8 %collective-permute-start = (bf16[4,16,2048]{2,1,0:T(8,128)(2,1)S(1)}, bf16[4,16,2048]{2,1,0:T(8,128)(2,1)S(1)}, u32[]{:S(2)}, u32[]{:S(2)}) collective-permute-start(bf16[4,16,2048]{2,1,0:T(8,128)(2,1)S(1)} %get-tuple-element.8), channel_id=1, source_target_pairs={{1,2},{3,4},{5,6},{7,8},{9,10},{11,12},{13,14},{15,16},{17,18},{19... | collective-permute-start | bytes 786440 | tf_op jit(solution)/shard_map/ppermute | solution.py:283
  25.0 9.2 %collective-permute-start.2 = (f32[32,256]{1,0:T(8,128)S(1)}, f32[32,256]{1,0:T(8,128)S(1)}, u32[]{:S(2)}, u32[]{:S(2)}) collective-permute-start(f32[32,256]{1,0:T(8,128)S(1)} %merge_other.1), channel_id=1, source_target_pairs={{0,128},{32,160},{64,192},{96,224},{128,0},{160,32},{192,64},{224,... | collective-permute-start | bytes 98312 | tf_op jit(solution)/shard_map/ppermute | solution.py:335
